TPU v7x, 32 devices: a whole 2x2x4 slice. The times are simulated.
32 devices in a mesh: groups: 2 (over x), seq: 16 (over z, y, core).
Axes of the slice: x: 2, y: 2, z: 4, core: 2. Of those that a mesh axis runs over, the one named last changes fastest.
Arguments:
- candidates: bfloat16 [32, 256, 256], P('groups', 'seq'), parts along dimension 0, may hold values from -110 to 110
- codes: int32 [32, 2048, 256], P('groups', 'seq'), parts along dimension 0, may hold values from -2147483648 to 2147483647
- scale_index: int32 [32, 8192], P('groups', 'seq'), parts along dimension 0, may hold values from 0 to 255
- lengths: int32 [32], P('groups'), parts along dimension 0, may hold values from 128 to 8192, as said below
- scale_table: float32 [256], replicated, may hold values from 0.004 to 0.04
- query_weight: bfloat16 [256, 256], replicated, may hold values from -0.375 to 0.375
- key_weight: bfloat16 [256, 256], replicated, may hold values from -0.375 to 0.375
- value_weight: bfloat16 [256, 256], replicated, may hold values from -0.375 to 0.375
- out_weight: bfloat16 [256, 256], replicated, may hold values from -0.375 to 0.375
- norm_gain: float32 [256], replicated, may hold values from 0.1 to 1.9
- hidden_weight: bfloat16 [256, 512], replicated, may hold values from -0.375 to 0.375
- hidden_bias: float32 [512], replicated, may hold values from -4 to 4
- score_weight: bfloat16 [512], replicated, may hold values from -0.25 to 0.25
Outputs:
- interest: bfloat16 [32, 256, 256], P('groups', 'seq'), parts along dimension 0
- logits: float32 [32, 256], P('groups', 'seq'), parts along dimension 0
There are 2 independent parts, one for each index of `groups`. A program takes and returns all parts, laid end to end along the dimension named above; an argument that names none is the same for every part. Nothing has to cross between parts.
Inputs may be any that keep to these rules, and one draw needn't show every extreme that they name: `lengths`: each user's history length is a multiple of 128; in every draw some user's length is 8192.
All inputs are finite; a program needn't handle non-finite values.
Results may differ from a plain program's by a relative error of at most 0.02.
The roundings to bfloat16 on the way count: a program that leaves them out, or rounds other values in their place, can miss the bound.
Values may be sent and summed in bfloat16 or wider, within the bound.
A program may use at most 128 MiB of HBM per device.

v0:
```python
import math
import jax
import jax.numpy as jnp
from jax import lax
from jax.sharding import PartitionSpec as P

HEADS = 4
NEG_FILL = -1e30


def unpack_codes(words):
    byte_rows = [jnp.right_shift(jnp.left_shift(words, 24 - 8 * k), 24) for k in range(4)]
    stacked = jnp.stack(byte_rows, axis=1)
    return stacked.reshape(words.shape[0] * 4, words.shape[1])


def score_block(query_rows, key_rows, live_row):
    cand_rows, model_width = query_rows.shape
    head_size = model_width // HEADS
    split_query = query_rows.reshape(cand_rows, HEADS, head_size)
    split_keys = key_rows.reshape(key_rows.shape[0], HEADS, head_size)
    scores = jnp.einsum("chd,khd->hck", split_query, split_keys, preferred_element_type=jnp.float32)
    scores = scores * (1.0 / math.sqrt(head_size))
    return jnp.where(live_row[None, None, :], scores, NEG_FILL)


def exp_weights(scores, live_row, peak_rows):
    return jnp.where(live_row[None, None, :], jnp.exp(scores - peak_rows[:, :, None]), 0.0)


def weighted_rows(weights, value_rows):
    head_count, cand_rows, key_count = weights.shape
    split_values = value_rows.reshape(key_count, head_count, -1)
    blended = jnp.einsum(
        "hck,khd->chd",
        weights.astype(jnp.bfloat16),
        split_values,
        preferred_element_type=jnp.float32,
    )
    return blended.reshape(cand_rows, -1)


def local_partials(user_item):
    query_rows, key_rows, value_rows, live_row = user_item
    scores = score_block(query_rows, key_rows, live_row)
    peak_rows = jnp.max(scores, axis=2)
    weights = exp_weights(scores, live_row, peak_rows)
    return (weighted_rows(weights, value_rows), jnp.sum(weights, axis=2), peak_rows)


def on_device(
    candidates,
    codes,
    scale_index,
    lengths,
    scale_table,
    query_weight,
    key_weight,
    value_weight,
    out_weight,
    norm_gain,
    hidden_weight,
    hidden_bias,
    score_weight,
):
    user_count, cand_local, model_width = candidates.shape
    hist_local = scale_index.shape[1]
    head_size = model_width // HEADS
    own_queries = jnp.einsum(
        "ucd,de->uce", candidates, query_weight, preferred_element_type=jnp.float32
    ).astype(jnp.bfloat16)
    queries = lax.all_gather(own_queries, "seq", axis=1, tiled=True)
    offset = lax.axis_index("seq") * hist_local
    places = offset + jnp.arange(hist_local, dtype=jnp.int32)
    live_mask = places[None, :] < lengths[:, None]
    levels = jnp.arange(scale_table.shape[0], dtype=jnp.int32)

    def project(user_item):
        word_rows, index_rows = user_item
        code_rows = unpack_codes(word_rows)
        row_scales = jnp.sum(
            jnp.where(index_rows[:, None] == levels[None, :], scale_table[None, :], 0.0), axis=1
        )
        history = (code_rows.astype(jnp.float32) * row_scales[:, None]).astype(jnp.bfloat16)
        key_rows = jnp.dot(history, key_weight, preferred_element_type=jnp.float32).astype(
            jnp.bfloat16
        )
        value_rows = jnp.dot(history, value_weight, preferred_element_type=jnp.float32).astype(
            jnp.bfloat16
        )
        return (key_rows, value_rows)

    all_keys, all_values = lax.map(project, (codes, scale_index))
    numerators, totals, peak_rows = lax.map(
        local_partials, (queries, all_keys, all_values, live_mask)
    )
    got_numerators = lax.all_to_all(
        numerators[None].astype(jnp.bfloat16), "seq", split_axis=2, concat_axis=0, tiled=True
    ).astype(jnp.float32)
    got_peaks, got_totals = (
        lax.all_to_all(peak_rows[None], "seq", split_axis=3, concat_axis=0, tiled=True),
        lax.all_to_all(totals[None], "seq", split_axis=3, concat_axis=0, tiled=True),
    )
    global_peaks = jnp.max(got_peaks, axis=0)
    factor = jnp.exp(got_peaks - global_peaks[None])
    totals = jnp.sum(factor * got_totals, axis=0)
    sources = got_numerators.shape[0]
    scaled = (
        got_numerators.reshape(sources, user_count, cand_local, HEADS, head_size)
        * jnp.transpose(factor, (0, 1, 3, 2))[..., None]
    )
    numerators = jnp.sum(scaled, axis=0).reshape(user_count, cand_local, model_width)
    split_numer = numerators.reshape(user_count, cand_local, HEADS, head_size)
    attended = (
        (split_numer / jnp.transpose(totals, (0, 2, 1))[..., None])
        .reshape(user_count, cand_local, model_width)
        .astype(jnp.bfloat16)
    )
    interest = jnp.einsum(
        "ucd,de->uce", attended, out_weight, preferred_element_type=jnp.float32
    ).astype(jnp.bfloat16)
    floats = interest.astype(jnp.float32)
    normed = (
        floats * lax.rsqrt(jnp.mean(floats * floats, axis=2, keepdims=True) + 1e-06) * norm_gain
    ).astype(jnp.bfloat16)
    hidden = jax.nn.silu(
        jnp.einsum("ucd,dh->uch", normed, hidden_weight, preferred_element_type=jnp.float32)
        + hidden_bias
    ).astype(jnp.bfloat16)
    logits = jnp.einsum("uch,h->uc", hidden, score_weight, preferred_element_type=jnp.float32)
    return (interest, logits)


def solution(mesh):
    placed = (
        P("groups", "seq", None),
        P("groups", "seq", None),
        P("groups", "seq"),
        P("groups"),
        P(),
        P(),
        P(),
        P(),
        P(),
        P(),
        P(),
        P(),
        P(),
    )
    return jax.shard_map(
        on_device,
        mesh=mesh,
        in_specs=placed,
        out_specs=(P("groups", "seq", None), P("groups", "seq")),
        check_vma=False,
    )
```

profile of v0, /device:TPU:13, one launch (start us, length us, event | category | flops | bytes accessed | tf_op | source)
XLA Modules:
  0.0 369.4 jit_solution(11931711030557221657)
XLA Ops:
  9.1 80.3 %while.28 = (s32[]{:T(128)}, bf16[16,512,256]{2,1,0:T(8,128)(2,1)}, bf16[16,512,256]{2,1,0:T(8,128)(2,1)}, s32[16,128,256]{2,1,0:T(8,128)}, s32[16,512]{1,0:T(8,...) while((s32[]{:T(128)}, bf16[16,512,256]{2,1,0:T(8,128)(2,1)}, ...), condition=%wide.region_2.3_spmd.clone, body=%wide.region_0.2_spmd.clone.sunk | while | flops 136183296 | bytes 5916857 | solution.py:93
  89.5 191.5 %while.27 = (s32[]{:T(128)}, bf16[16,256,256]{2,0,1:T(8,128)(2,1)}, f32[16,4,256]{2,1,0:T(4,128)S(1)}, f32[16,4,256]{2,1,0:T(4,128)S(1)}, bf16[16,512,256]{2,1,0...) while((s32[]{:T(128)}, bf16[16,256,256]{2,0,1:T(8,128)(2,1)}, ...), condition=%wide.region_6.7_spmd, body=%wide.region_3.6_spmd.sunk | while | flops 141031424 | bytes 10259069 | solution.py:94
  94.8 6.6 %dynamic_update_slice.29 = bf16[16,256,256]{2,0,1:T(8,128)(2,1)} dynamic-update-slice(bf16[16,256,256]{2,0,1:T(8,128)(2,1)} %get-tuple-element.385, bf16[1,256,256]{2,0,1:T(2,128)(2,1)S(1)} %copy.82, s32[]{:T(128)} %get-tuple-element.384, s32[]{:T(128)} %constant.40.clone.1..sunk, s32[]{:T(128)} %constant.40.clone.1..sunk) | dynamic-update-slice | bytes 262148 | tf_op jit(solution)/shard_map/while/body/jit(dynamic_update_index_in_dim)/dynamic_update_slice | solution.py:94
  106.8 6.6 %dynamic_update_slice.29 = bf16[16,256,256]{2,0,1:T(8,128)(2,1)} dynamic-update-slice(bf16[16,256,256]{2,0,1:T(8,128)(2,1)} %get-tuple-element.385, bf16[1,256,256]{2,0,1:T(2,128)(2,1)S(1)} %copy.82, s32[]{:T(128)} %get-tuple-element.384, s32[]{:T(128)} %constant.40.clone.1..sunk, s32[]{:T(128)} %constant.40.clone.1..sunk) | dynamic-update-slice | bytes 262148 | tf_op jit(solution)/shard_map/while/body/jit(dynamic_update_index_in_dim)/dynamic_update_slice | solution.py:94
  118.8 6.6 %dynamic_update_slice.29 = bf16[16,256,256]{2,0,1:T(8,128)(2,1)} dynamic-update-slice(bf16[16,256,256]{2,0,1:T(8,128)(2,1)} %get-tuple-element.385, bf16[1,256,256]{2,0,1:T(2,128)(2,1)S(1)} %copy.82, s32[]{:T(128)} %get-tuple-element.384, s32[]{:T(128)} %constant.40.clone.1..sunk, s32[]{:T(128)} %constant.40.clone.1..sunk) | dynamic-update-slice | bytes 262148 | tf_op jit(solution)/shard_map/while/body/jit(dynamic_update_index_in_dim)/dynamic_update_slice | solution.py:94
  130.8 6.6 %dynamic_update_slice.29 = bf16[16,256,256]{2,0,1:T(8,128)(2,1)} dynamic-update-slice(bf16[16,256,256]{2,0,1:T(8,128)(2,1)} %get-tuple-element.385, bf16[1,256,256]{2,0,1:T(2,128)(2,1)S(1)} %copy.82, s32[]{:T(128)} %get-tuple-element.384, s32[]{:T(128)} %constant.40.clone.1..sunk, s32[]{:T(128)} %constant.40.clone.1..sunk) | dynamic-update-slice | bytes 262148 | tf_op jit(solution)/shard_map/while/body/jit(dynamic_update_index_in_dim)/dynamic_update_slice | solution.py:94
  142.7 6.6 %dynamic_update_slice.29 = bf16[16,256,256]{2,0,1:T(8,128)(2,1)} dynamic-update-slice(bf16[16,256,256]{2,0,1:T(8,128)(2,1)} %get-tuple-element.385, bf16[1,256,256]{2,0,1:T(2,128)(2,1)S(1)} %copy.82, s32[]{:T(128)} %get-tuple-element.384, s32[]{:T(128)} %constant.40.clone.1..sunk, s32[]{:T(128)} %constant.40.clone.1..sunk) | dynamic-update-slice | bytes 262148 | tf_op jit(solution)/shard_map/while/body/jit(dynamic_update_index_in_dim)/dynamic_update_slice | solution.py:94
  154.7 6.6 %dynamic_update_slice.29 = bf16[16,256,256]{2,0,1:T(8,128)(2,1)} dynamic-update-slice(bf16[16,256,256]{2,0,1:T(8,128)(2,1)} %get-tuple-element.385, bf16[1,256,256]{2,0,1:T(2,128)(2,1)S(1)} %copy.82, s32[]{:T(128)} %get-tuple-element.384, s32[]{:T(128)} %constant.40.clone.1..sunk, s32[]{:T(128)} %constant.40.clone.1..sunk) | dynamic-update-slice | bytes 262148 | tf_op jit(solution)/shard_map/while/body/jit(dynamic_update_index_in_dim)/dynamic_update_slice | solution.py:94
  166.7 6.6 %dynamic_update_slice.29 = bf16[16,256,256]{2,0,1:T(8,128)(2,1)} dynamic-update-slice(bf16[16,256,256]{2,0,1:T(8,128)(2,1)} %get-tuple-element.385, bf16[1,256,256]{2,0,1:T(2,128)(2,1)S(1)} %copy.82, s32[]{:T(128)} %get-tuple-element.384, s32[]{:T(128)} %constant.40.clone.1..sunk, s32[]{:T(128)} %constant.40.clone.1..sunk) | dynamic-update-slice | bytes 262148 | tf_op jit(solution)/shard_map/while/body/jit(dynamic_update_index_in_dim)/dynamic_update_slice | solution.py:94
  178.7 6.6 %dynamic_update_slice.29 = bf16[16,256,256]{2,0,1:T(8,128)(2,1)} dynamic-update-slice(bf16[16,256,256]{2,0,1:T(8,128)(2,1)} %get-tuple-element.385, bf16[1,256,256]{2,0,1:T(2,128)(2,1)S(1)} %copy.82, s32[]{:T(128)} %get-tuple-element.384, s32[]{:T(128)} %constant.40.clone.1..sunk, s32[]{:T(128)} %constant.40.clone.1..sunk) | dynamic-update-slice | bytes 262148 | tf_op jit(solution)/shard_map/while/body/jit(dynamic_update_index_in_dim)/dynamic_update_slice | solution.py:94
  190.6 6.6 %dynamic_update_slice.29 = bf16[16,256,256]{2,0,1:T(8,128)(2,1)} dynamic-update-slice(bf16[16,256,256]{2,0,1:T(8,128)(2,1)} %get-tuple-element.385, bf16[1,256,256]{2,0,1:T(2,128)(2,1)S(1)} %copy.82, s32[]{:T(128)} %get-tuple-element.384, s32[]{:T(128)} %constant.40.clone.1..sunk, s32[]{:T(128)} %constant.40.clone.1..sunk) | dynamic-update-slice | bytes 262148 | tf_op jit(solution)/shard_map/while/body/jit(dynamic_update_index_in_dim)/dynamic_update_slice | solution.py:94
  202.6 6.6 %dynamic_update_slice.29 = bf16[16,256,256]{2,0,1:T(8,128)(2,1)} dynamic-update-slice(bf16[16,256,256]{2,0,1:T(8,128)(2,1)} %get-tuple-element.385, bf16[1,256,256]{2,0,1:T(2,128)(2,1)S(1)} %copy.82, s32[]{:T(128)} %get-tuple-element.384, s32[]{:T(128)} %constant.40.clone.1..sunk, s32[]{:T(128)} %constant.40.clone.1..sunk) | dynamic-update-slice | bytes 262148 | tf_op jit(solution)/shard_map/while/body/jit(dynamic_update_index_in_dim)/dynamic_update_slice | solution.py:94
  214.6 6.6 %dynamic_update_slice.29 = bf16[16,256,256]{2,0,1:T(8,128)(2,1)} dynamic-update-slice(bf16[16,256,256]{2,0,1:T(8,128)(2,1)} %get-tuple-element.385, bf16[1,256,256]{2,0,1:T(2,128)(2,1)S(1)} %copy.82, s32[]{:T(128)} %get-tuple-element.384, s32[]{:T(128)} %constant.40.clone.1..sunk, s32[]{:T(128)} %constant.40.clone.1..sunk) | dynamic-update-slice | bytes 262148 | tf_op jit(solution)/shard_map/while/body/jit(dynamic_update_index_in_dim)/dynamic_update_slice | solution.py:94
  226.5 6.6 %dynamic_update_slice.29 = bf16[16,256,256]{2,0,1:T(8,128)(2,1)} dynamic-update-slice(bf16[16,256,256]{2,0,1:T(8,128)(2,1)} %get-tuple-element.385, bf16[1,256,256]{2,0,1:T(2,128)(2,1)S(1)} %copy.82, s32[]{:T(128)} %get-tuple-element.384, s32[]{:T(128)} %constant.40.clone.1..sunk, s32[]{:T(128)} %constant.40.clone.1..sunk) | dynamic-update-slice | bytes 262148 | tf_op jit(solution)/shard_map/while/body/jit(dynamic_update_index_in_dim)/dynamic_update_slice | solution.py:94
  238.5 6.6 %dynamic_update_slice.29 = bf16[16,256,256]{2,0,1:T(8,128)(2,1)} dynamic-update-slice(bf16[16,256,256]{2,0,1:T(8,128)(2,1)} %get-tuple-element.385, bf16[1,256,256]{2,0,1:T(2,128)(2,1)S(1)} %copy.82, s32[]{:T(128)} %get-tuple-element.384, s32[]{:T(128)} %constant.40.clone.1..sunk, s32[]{:T(128)} %constant.40.clone.1..sunk) | dynamic-update-slice | bytes 262148 | tf_op jit(solution)/shard_map/while/body/jit(dynamic_update_index_in_dim)/dynamic_update_slice | solution.py:94
  250.5 6.6 %dynamic_update_slice.29 = bf16[16,256,256]{2,0,1:T(8,128)(2,1)} dynamic-update-slice(bf16[16,256,256]{2,0,1:T(8,128)(2,1)} %get-tuple-element.385, bf16[1,256,256]{2,0,1:T(2,128)(2,1)S(1)} %copy.82, s32[]{:T(128)} %get-tuple-element.384, s32[]{:T(128)} %constant.40.clone.1..sunk, s32[]{:T(128)} %constant.40.clone.1..sunk) | dynamic-update-slice | bytes 262148 | tf_op jit(solution)/shard_map/while/body/jit(dynamic_update_index_in_dim)/dynamic_update_slice | solution.py:94
  262.4 6.6 %dynamic_update_slice.29 = bf16[16,256,256]{2,0,1:T(8,128)(2,1)} dynamic-update-slice(bf16[16,256,256]{2,0,1:T(8,128)(2,1)} %get-tuple-element.385, bf16[1,256,256]{2,0,1:T(2,128)(2,1)S(1)} %copy.82, s32[]{:T(128)} %get-tuple-element.384, s32[]{:T(128)} %constant.40.clone.1..sunk, s32[]{:T(128)} %constant.40.clone.1..sunk) | dynamic-update-slice | bytes 262148 | tf_op jit(solution)/shard_map/while/body/jit(dynamic_update_index_in_dim)/dynamic_update_slice | solution.py:94
  274.4 6.6 %dynamic_update_slice.29 = bf16[16,256,256]{2,0,1:T(8,128)(2,1)} dynamic-update-slice(bf16[16,256,256]{2,0,1:T(8,128)(2,1)} %get-tuple-element.385, bf16[1,256,256]{2,0,1:T(2,128)(2,1)S(1)} %copy.82, s32[]{:T(128)} %get-tuple-element.384, s32[]{:T(128)} %constant.40.clone.1..sunk, s32[]{:T(128)} %constant.40.clone.1..sunk) | dynamic-update-slice | bytes 262148 | tf_op jit(solution)/shard_map/while/body/jit(dynamic_update_index_in_dim)/dynamic_update_slice | solution.py:94
  282.4 6.5 %all-to-all-start.1 = ((f32[16,1,1024]{2,1,0:T(1,128)}), f32[16,1,1024]{2,1,0:T(1,128)S(1)}, u32[]{:S(2)}, u32[]{:S(2)}) async-start(f32[16,1,1024]{2,1,0:T(1,128)} %reshape.134), calls=%async_computation.1 | async-start | bytes 131072 | tf_op jit(solution)/shard_map/all_to_all | solution.py:101
  293.2 9.5 %all_to_all.45 = f32[16,1,1024]{2,1,0:T(1,128)S(1)} all-to-all(f32[16,1,1024]{2,1,0:T(1,128)S(1)} %reshape.136), channel_id=1, replica_groups=mesh['groups'=2,'seq'=16] {'seq'}, dimensions={0} | all-to-all | bytes 131072 | tf_op jit(solution)/shard_map/all_to_all | solution.py:102
  302.6 7.1 %all-to-all-start = ((bf16[1,16,256,256]{3,1,0,2:T(8,128)(2,1)}), bf16[1,16,256,256]{3,1,0,2:T(8,128)(2,1)}, u32[]{:S(2)}, u32[]{:S(2)}) async-start(bf16[1,16,256,256]{3,1,0,2:T(8,128)(2,1)} %bitcast.75), calls=%async_computation | async-start | bytes 4194304 | tf_op jit(solution)/shard_map/all_to_all | solution.py:97
  316.1 7.0 %mul.52 = f32[16,16,16,4,64]{4,3,2,0,1:T(4,128)} broadcast(f32[16,16,16,4]{3,2,0,1:T(8,128)S(1)} %copy.56), dimensions={0,1,2,3} | broadcast | bytes 4259840 | tf_op jit(solution)/shard_map/mul | solution.py:109
  323.1 8.6 %mul.53 = f32[16,1,16,16,256]{4,3,0,2,1:T(8,128)} reshape(f32[16,16,16,4,64]{4,3,2,0,1:T(4,128)} %mul.52) | data formatting | bytes 8388608 | tf_op jit(solution)/shard_map/mul | solution.py:109
  332.6 24.7 %all-to-all-done = bf16[1,16,256,256]{3,1,0,2:T(8,128)(2,1)} async-done(((bf16[1,16,256,256]{3,1,0,2:T(8,128)(2,1)}), bf16[1,16,256,256]{3,1,0,2:T(8,128)(2,1)}, u32[]{:S(2)}, u32[]{:S(2)}) %all-to-all-start) | async-done | bytes 2097184 | tf_op jit(solution)/shard_map/all_to_all | solution.py:97
  (471 shorter events, 184.3 us)
Async XLA Ops:
  7.2 354.1 %copy-start = (bf16[256,512]{1,0:T(8,128)(2,1)S(1)}, bf16[256,512]{1,0:T(8,128)(2,1)}, u32[]{:S(2)}) copy-start(bf16[256,512]{1,0:T(8,128)(2,1)} %param.27) | copy-start | bytes 786436
  7.2 82.3 %all-gather.2.cloned.1.call-start = ((), (), s32[]{:S(2)}) async-start(), calls=%async_computation.3 | async-start | bytes 2228224 | tf_op jit(solution)/shard_map/all_gather | solution.py:72
  9.1 80.3 %copy-start.7 = (s32[16]{0:T(128)S(1)}, s32[16]{0:T(128)}, u32[]{:S(2)}) copy-start(s32[16]{0:T(128)} %param.20) | copy-start | bytes 196
  9.2 4.0 %copy-start.2 = (bf16[256,256]{1,0:T(8,128)(2,1)S(1)}, bf16[256,256]{1,0:T(8,128)(2,1)}, u32[]{:S(2)}) copy-start(bf16[256,256]{1,0:T(8,128)(2,1)} %get-tuple-element.371) | copy-start | bytes 393220 | tf_op jit(solution)/shard_map/while
  14.2 4.0 %copy-start.2 = (bf16[256,256]{1,0:T(8,128)(2,1)S(1)}, bf16[256,256]{1,0:T(8,128)(2,1)}, u32[]{:S(2)}) copy-start(bf16[256,256]{1,0:T(8,128)(2,1)} %get-tuple-element.371) | copy-start | bytes 393220 | tf_op jit(solution)/shard_map/while
  19.1 4.0 %copy-start.2 = (bf16[256,256]{1,0:T(8,128)(2,1)S(1)}, bf16[256,256]{1,0:T(8,128)(2,1)}, u32[]{:S(2)}) copy-start(bf16[256,256]{1,0:T(8,128)(2,1)} %get-tuple-element.371) | copy-start | bytes 393220 | tf_op jit(solution)/shard_map/while
  24.2 4.0 %copy-start.2 = (bf16[256,256]{1,0:T(8,128)(2,1)S(1)}, bf16[256,256]{1,0:T(8,128)(2,1)}, u32[]{:S(2)}) copy-start(bf16[256,256]{1,0:T(8,128)(2,1)} %get-tuple-element.371) | copy-start | bytes 393220 | tf_op jit(solution)/shard_map/while
  29.2 4.0 %copy-start.2 = (bf16[256,256]{1,0:T(8,128)(2,1)S(1)}, bf16[256,256]{1,0:T(8,128)(2,1)}, u32[]{:S(2)}) copy-start(bf16[256,256]{1,0:T(8,128)(2,1)} %get-tuple-element.371) | copy-start | bytes 393220 | tf_op jit(solution)/shard_map/while
  34.2 4.0 %copy-start.2 = (bf16[256,256]{1,0:T(8,128)(2,1)S(1)}, bf16[256,256]{1,0:T(8,128)(2,1)}, u32[]{:S(2)}) copy-start(bf16[256,256]{1,0:T(8,128)(2,1)} %get-tuple-element.371) | copy-start | bytes 393220 | tf_op jit(solution)/shard_map/while
  39.2 4.0 %copy-start.2 = (bf16[256,256]{1,0:T(8,128)(2,1)S(1)}, bf16[256,256]{1,0:T(8,128)(2,1)}, u32[]{:S(2)}) copy-start(bf16[256,256]{1,0:T(8,128)(2,1)} %get-tuple-element.371) | copy-start | bytes 393220 | tf_op jit(solution)/shard_map/while
  44.3 4.0 %copy-start.2 = (bf16[256,256]{1,0:T(8,128)(2,1)S(1)}, bf16[256,256]{1,0:T(8,128)(2,1)}, u32[]{:S(2)}) copy-start(bf16[256,256]{1,0:T(8,128)(2,1)} %get-tuple-element.371) | copy-start | bytes 393220 | tf_op jit(solution)/shard_map/while
  49.3 3.1 copy-start.3
  49.3 4.1 %copy-start.2 = (bf16[256,256]{1,0:T(8,128)(2,1)S(1)}, bf16[256,256]{1,0:T(8,128)(2,1)}, u32[]{:S(2)}) copy-start(bf16[256,256]{1,0:T(8,128)(2,1)} %get-tuple-element.371) | copy-start | bytes 393220 | tf_op jit(solution)/shard_map/while
  54.3 4.0 %copy-start.2 = (bf16[256,256]{1,0:T(8,128)(2,1)S(1)}, bf16[256,256]{1,0:T(8,128)(2,1)}, u32[]{:S(2)}) copy-start(bf16[256,256]{1,0:T(8,128)(2,1)} %get-tuple-element.371) | copy-start | bytes 393220 | tf_op jit(solution)/shard_map/while
  59.3 4.0 %copy-start.2 = (bf16[256,256]{1,0:T(8,128)(2,1)S(1)}, bf16[256,256]{1,0:T(8,128)(2,1)}, u32[]{:S(2)}) copy-start(bf16[256,256]{1,0:T(8,128)(2,1)} %get-tuple-element.371) | copy-start | bytes 393220 | tf_op jit(solution)/shard_map/while
  64.4 4.0 %copy-start.2 = (bf16[256,256]{1,0:T(8,128)(2,1)S(1)}, bf16[256,256]{1,0:T(8,128)(2,1)}, u32[]{:S(2)}) copy-start(bf16[256,256]{1,0:T(8,128)(2,1)} %get-tuple-element.371) | copy-start | bytes 393220 | tf_op jit(solution)/shard_map/while
  69.4 4.0 %copy-start.2 = (bf16[256,256]{1,0:T(8,128)(2,1)S(1)}, bf16[256,256]{1,0:T(8,128)(2,1)}, u32[]{:S(2)}) copy-start(bf16[256,256]{1,0:T(8,128)(2,1)} %get-tuple-element.371) | copy-start | bytes 393220 | tf_op jit(solution)/shard_map/while
  74.4 4.0 %copy-start.2 = (bf16[256,256]{1,0:T(8,128)(2,1)S(1)}, bf16[256,256]{1,0:T(8,128)(2,1)}, u32[]{:S(2)}) copy-start(bf16[256,256]{1,0:T(8,128)(2,1)} %get-tuple-element.371) | copy-start | bytes 393220 | tf_op jit(solution)/shard_map/while
  79.4 4.0 %copy-start.2 = (bf16[256,256]{1,0:T(8,128)(2,1)S(1)}, bf16[256,256]{1,0:T(8,128)(2,1)}, u32[]{:S(2)}) copy-start(bf16[256,256]{1,0:T(8,128)(2,1)} %get-tuple-element.371) | copy-start | bytes 393220 | tf_op jit(solution)/shard_map/while
  84.4 4.0 %copy-start.2 = (bf16[256,256]{1,0:T(8,128)(2,1)S(1)}, bf16[256,256]{1,0:T(8,128)(2,1)}, u32[]{:S(2)}) copy-start(bf16[256,256]{1,0:T(8,128)(2,1)} %get-tuple-element.371) | copy-start | bytes 393220 | tf_op jit(solution)/shard_map/while
  282.4 10.8 %all-to-all-start.1 = ((f32[16,1,1024]{2,1,0:T(1,128)}), f32[16,1,1024]{2,1,0:T(1,128)S(1)}, u32[]{:S(2)}, u32[]{:S(2)}) async-start(f32[16,1,1024]{2,1,0:T(1,128)} %reshape.134), calls=%async_computation.1 | async-start | bytes 131072 | tf_op jit(solution)/shard_map/all_to_all | solution.py:101
  302.6 7.1 %copy-start.6 = (bf16[512]{0:T(512)(128)(2,1)S(1)}, bf16[512]{0:T(512)(128)(2,1)}, u32[]{:S(2)}) copy-start(bf16[512]{0:T(512)(128)(2,1)} %param.29) | copy-start | bytes 3076
  302.6 54.6 %all-to-all-start = ((bf16[1,16,256,256]{3,1,0,2:T(8,128)(2,1)}), bf16[1,16,256,256]{3,1,0,2:T(8,128)(2,1)}, u32[]{:S(2)}, u32[]{:S(2)}) async-start(bf16[1,16,256,256]{3,1,0,2:T(8,128)(2,1)} %bitcast.75), calls=%async_computation | async-start | bytes 4194304 | tf_op jit(solution)/shard_map/all_to_all | solution.py:97
  323.1 8.6 %copy-start.4 = (f32[16,4,16]{2,1,0:T(4,128)S(1)}, f32[16,4,16]{2,1,0:T(4,128)}, u32[]{:S(2)}) copy-start(f32[16,4,16]{2,1,0:T(4,128)} %get-tuple-element.229) | copy-start | bytes 12292
  (36 other events, 97.5 us)
Sparse Core Ops, SparseCore 0:
  10.7 42.2 all-gather.1
where the time goes:
time: 374 us; the launch traced here: 369 us
  local copies, waits for them, and re-layouts  217 us (58%)
  matrix products  54.2 us (14%)
  other arithmetic  31.3 us (8%)
  waiting for transfers between devices  28.2 us (8%)
  between operations  14.2 us (4%)
  starting transfers between devices  13.6 us (4%)
  blocking collectives  9.45 us (3%)
    dynamic_update_slice x48, local copies, waits for them, and re-layouts, on_device(): lax.map(local_partials, (queries, all_keys, all_values, live_mask))  109 us
    dynamic_slice x112, local copies, waits for them, and re-layouts, on_device(): lax.map(local_partials, (queries, all_keys, all_values, live_mask))  52.3 us
    dynamic_slice x32, local copies, waits for them, and re-layouts, on_device(): all_keys, all_values = lax.map(project, (codes, scale_index))  27 us
    all_to_all x1, waiting for transfers between devices, on_device(): lax.all_to_all(numerators[None].astype(jnp.bfloat16), 'seq', split_axis=2...  24.7 us
    dot_general x16, matrix products, project(): jnp.dot(history, value_weight, preferred_element_type=jnp.float32)  15.9 us
    dot_general x16, matrix products, project(): jnp.dot(history, key_weight, preferred_element_type=jnp.float32)  15.8 us
    mul x2, local copies, waits for them, and re-layouts, on_device(): got_numerators.reshape(sources, user_count, cand_local, HEADS, head_size)  15.6 us
    reduce_sum x16, other arithmetic, local_partials(): jnp.sum(weights, axis=2)  10.1 us
  transfers between devices with their start and end apart: 3, of which 2 were waited for; matrix products, arithmetic and copies ran while one was open for 28% of the time, Pallas kernels for 0%

commit v1 on v0

--- a/solution.py
+++ b/solution.py
@@ -94,8 +94,16 @@
     numerators, totals, peak_rows = lax.map(
         local_partials, (queries, all_keys, all_values, live_mask)
     )
-    got_numerators = lax.all_to_all(
-        numerators[None].astype(jnp.bfloat16), "seq", split_axis=2, concat_axis=0, tiled=True
+    got_numerators = jnp.concatenate(
+        lax.all_to_all(
+            jnp.stack(
+                jnp.split(numerators[None].astype(jnp.bfloat16), lax.axis_size("seq"), axis=2)
+            ),
+            "seq",
+            0,
+            0,
+        ),
+        axis=0,
     ).astype(jnp.float32)
     got_peaks, got_totals = (
         lax.all_to_all(peak_rows[None], "seq", split_axis=3, concat_axis=0, tiled=True),

time: 374 us -> 295 us (0.79)
  local copies, waits for them, and re-layouts: 217 us -> 136 us
  blocking collectives: 9.45 us -> 0 us
  starting transfers between devices: 13.6 us -> 19.5 us
  waiting for transfers between devices: 28.2 us -> 32.1 us
    dynamic_update_slice x48, local copies, waits for them, and re-layouts: 109 us -> 12.4 us  [on_device(): lax.map(local_partials, (queries, all_keys, all_values, live_mask))]
    unnamed x25 -> x39, local copies, waits for them, and re-layouts: 2.97 us -> 21.5 us
    all_to_all x1 -> x0, blocking collectives: 9.45 us -> none  [on_device(): lax.all_to_all(totals[None], 'seq', split_axis=3, concat_axis=0, tiled=True)]
    all_to_all x1 -> x2, starting transfers between devices: 7.07 us -> 13 us  [the longest x1 6.94 us: on_device(): lax.all_to_all(jnp.stack(jnp.split(numerators[None].astype(jnp.bfloat16),...]
    all_to_all x1 -> x2, waiting for transfers between devices: 24.7 us -> 29.8 us  [the longest x1 26.1 us: on_device(): lax.all_to_all(jnp.stack(jnp.split(numerators[None].astype(jnp.bfloat16),...]
  transfers between devices with their start and end apart: 3 -> 4, of which waited for: 2 -> 3; matrix products, arithmetic and copies ran while one was open for 28% -> 36% of each run, Pallas kernels for 0% -> 0%
where the time goes in v1:
time: 295 us; the launch traced here: 292 us
  local copies, waits for them, and re-layouts  136 us (46%)
  matrix products  54.4 us (18%)
  other arithmetic  33.8 us (11%)
  waiting for transfers between devices  32.1 us (11%)
  starting transfers between devices  19.5 us (7%)
  between operations  14.3 us (5%)
    dynamic_slice x112, local copies, waits for them, and re-layouts, on_device(): lax.map(local_partials, (queries, all_keys, all_values, live_mask))  52.3 us
    dynamic_slice x32, local copies, waits for them, and re-layouts, on_device(): all_keys, all_values = lax.map(project, (codes, scale_index))  27 us
    all_to_all x1, waiting for transfers between devices, on_device(): lax.all_to_all(jnp.stack(jnp.split(numerators[None].astype(jnp.bfloat16),...  26.1 us
    unnamed x39, local copies, waits for them, and re-layouts  21.5 us
    dot_general x16, matrix products, project(): jnp.dot(history, value_weight, preferred_element_type=jnp.float32)  15.9 us
    dot_general x16, matrix products, project(): jnp.dot(history, key_weight, preferred_element_type=jnp.float32)  15.8 us
    mul x2, local copies, waits for them, and re-layouts, on_device(): got_numerators.reshape(sources, user_count, cand_local, HEADS, head_size)  15.6 us
    dynamic_update_slice x48, local copies, waits for them, and re-layouts, on_device(): lax.map(local_partials, (queries, all_keys, all_values, live_mask))  12.4 us
  transfers between devices with their start and end apart: 4, of which 3 were waited for; matrix products, arithmetic and copies ran while one was open for 36% of the time, Pallas kernels for 0%

profile of v1, /device:TPU:13, one launch (start us, length us, event | category | flops | bytes accessed | tf_op | source)
XLA Modules:
  0.0 291.5 jit_solution(3946409490598535527)
XLA Ops:
  7.2 1.8 convolution_convert_fusion.3
  9.1 80.3 %while.28 = (s32[]{:T(128)}, bf16[16,512,256]{2,1,0:T(8,128)(2,1)}, bf16[16,512,256]{2,1,0:T(8,128)(2,1)}, s32[16,128,256]{2,1,0:T(8,128)}, s32[16,512]{1,0:T(8,...) while((s32[]{:T(128)}, bf16[16,512,256]{2,1,0:T(8,128)(2,1)}, ...), condition=%wide.region_2.3_spmd.clone, body=%wide.region_0.2_spmd.clone.sunk | while | flops 136183296 | bytes 5916857 | solution.py:93
  89.5 94.8 %while.27 = (s32[]{:T(128)}, bf16[16,256,256]{2,1,0:T(8,128)(2,1)}, f32[16,4,256]{2,1,0:T(4,128)S(1)}, f32[16,4,256]{2,1,0:T(4,128)S(1)}, bf16[16,512,256]{2,1,0...) while((s32[]{:T(128)}, bf16[16,256,256]{2,1,0:T(8,128)(2,1)}, ...), condition=%wide.region_6.7_spmd, body=%wide.region_3.6_spmd.sunk | while | flops 141031424 | bytes 10259569 | solution.py:94
  184.3 1.7 fusion.44
  186.0 1.6 fusion.43
  187.5 1.6 fusion.42
  189.1 1.6 fusion.41
  190.7 1.6 fusion.40
  192.2 1.6 fusion.39
  193.8 1.6 fusion.38
  195.4 1.6 fusion.37
  201.2 1.0 reshape.132
  202.2 6.5 %all-to-all-start.1 = ((f32[16,1,1024]{2,1,0:T(1,128)}), f32[16,1,1024]{2,1,0:T(1,128)S(1)}, u32[]{:S(2)}, u32[]{:S(2)}) async-start(f32[16,1,1024]{2,1,0:T(1,128)} %reshape.132), calls=%async_computation.1 | async-start | bytes 131072 | tf_op jit(solution)/shard_map/all_to_all | solution.py:109
  209.0 1.1 reshape.134
  210.7 2.3 all-to-all-done.1
  213.0 6.0 %all-to-all-start.2 = ((f32[16,1,1024]{2,1,0:T(1,128)}), f32[16,1,1024]{2,1,0:T(1,128)S(1)}, u32[]{:S(2)}, u32[]{:S(2)}) async-start(f32[16,1,1024]{2,1,0:T(1,128)} %reshape.134), calls=%async_computation.2 | async-start | bytes 131072 | tf_op jit(solution)/shard_map/all_to_all | solution.py:110
  219.7 3.6 %all-to-all-done.2 = f32[16,1,1024]{2,1,0:T(1,128)S(1)} async-done(((f32[16,1,1024]{2,1,0:T(1,128)}), f32[16,1,1024]{2,1,0:T(1,128)S(1)}, u32[]{:S(2)}, u32[]{:S(2)}) %all-to-all-start.2) | async-done | bytes 65568 | tf_op jit(solution)/shard_map/all_to_all | solution.py:110
  223.3 6.9 %all-to-all-start = ((bf16[16,1,16,16,256]{4,3,2,1,0:T(8,128)(2,1)}), bf16[16,1,16,16,256]{4,3,2,1,0:T(8,128)(2,1)}, u32[]{:S(2)}, u32[]{:S(2)}) async-start(bf16[16,1,16,16,256]{4,3,2,1,0:T(8,128)(2,1)} %fusion.29), calls=%async_computation | async-start | bytes 4194304 | tf_op jit(solution)/shard_map/all_to_all | solution.py:98
  234.5 1.6 copy.55
  236.1 7.0 %mul.52 = f32[16,16,16,4,64]{4,3,2,1,0:T(4,128)} broadcast(f32[16,16,16,4]{3,2,1,0:T(8,128)S(1)} %copy.55), dimensions={0,1,2,3} | broadcast | bytes 4259840 | tf_op jit(solution)/shard_map/mul | solution.py:117
  243.1 8.6 %mul.53 = f32[16,1,16,16,256]{4,3,2,1,0:T(8,128)} reshape(f32[16,16,16,4,64]{4,3,2,1,0:T(4,128)} %mul.52) | data formatting | bytes 8388608 | tf_op jit(solution)/shard_map/mul | solution.py:117
  251.7 26.1 %all-to-all-done = bf16[16,1,16,16,256]{4,3,2,1,0:T(8,128)(2,1)} async-done(((bf16[16,1,16,16,256]{4,3,2,1,0:T(8,128)(2,1)}), bf16[16,1,16,16,256]{4,3,2,1,0:T(8,128)(2,1)}, u32[]{:S(2)}, u32[]{:S(2)}) %all-to-all-start) | async-done | bytes 2097184 | tf_op jit(solution)/shard_map/all_to_all | solution.py:98
  277.8 3.6 %multiply_reduce_fusion = f32[16,16,256]{2,1,0:T(8,128)S(1)} fusion(f32[16,1,16,16,256]{4,3,2,1,0:T(8,128)} %mul.53, bf16[16,1,16,16,256]{4,3,2,1,0:T(8,128)(2,1)} %all-to-all-done), kind=kLoop, calls=%fused_computation.34 | loop fusion | flops 3080192 | bytes 6553600 | tf_op jit(solution)/shard_map/reduce_sum | solution.py:120
  283.4 1.2 fusion.18
  (484 shorter events, 185.8 us)
Async XLA Ops:
  7.2 276.3 %copy-start = (bf16[256,512]{1,0:T(8,128)(2,1)S(1)}, bf16[256,512]{1,0:T(8,128)(2,1)}, u32[]{:S(2)}) copy-start(bf16[256,512]{1,0:T(8,128)(2,1)} %param.27) | copy-start | bytes 786436
  7.2 82.3 %all-gather.2.cloned.1.call-start = ((), (), s32[]{:S(2)}) async-start(), calls=%async_computation.3 | async-start | bytes 2228224 | tf_op jit(solution)/shard_map/all_gather | solution.py:72
  9.1 80.3 %copy-start.8 = (s32[16]{0:T(128)S(1)}, s32[16]{0:T(128)}, u32[]{:S(2)}) copy-start(s32[16]{0:T(128)} %param.20) | copy-start | bytes 196
  9.2 4.0 %copy-start.1 = (bf16[256,256]{1,0:T(8,128)(2,1)S(1)}, bf16[256,256]{1,0:T(8,128)(2,1)}, u32[]{:S(2)}) copy-start(bf16[256,256]{1,0:T(8,128)(2,1)} %get-tuple-element.371) | copy-start | bytes 393220 | tf_op jit(solution)/shard_map/while
  14.2 4.0 %copy-start.1 = (bf16[256,256]{1,0:T(8,128)(2,1)S(1)}, bf16[256,256]{1,0:T(8,128)(2,1)}, u32[]{:S(2)}) copy-start(bf16[256,256]{1,0:T(8,128)(2,1)} %get-tuple-element.371) | copy-start | bytes 393220 | tf_op jit(solution)/shard_map/while
  19.1 4.0 %copy-start.1 = (bf16[256,256]{1,0:T(8,128)(2,1)S(1)}, bf16[256,256]{1,0:T(8,128)(2,1)}, u32[]{:S(2)}) copy-start(bf16[256,256]{1,0:T(8,128)(2,1)} %get-tuple-element.371) | copy-start | bytes 393220 | tf_op jit(solution)/shard_map/while
  24.2 4.0 %copy-start.1 = (bf16[256,256]{1,0:T(8,128)(2,1)S(1)}, bf16[256,256]{1,0:T(8,128)(2,1)}, u32[]{:S(2)}) copy-start(bf16[256,256]{1,0:T(8,128)(2,1)} %get-tuple-element.371) | copy-start | bytes 393220 | tf_op jit(solution)/shard_map/while
  29.2 4.0 %copy-start.1 = (bf16[256,256]{1,0:T(8,128)(2,1)S(1)}, bf16[256,256]{1,0:T(8,128)(2,1)}, u32[]{:S(2)}) copy-start(bf16[256,256]{1,0:T(8,128)(2,1)} %get-tuple-element.371) | copy-start | bytes 393220 | tf_op jit(solution)/shard_map/while
  34.2 4.0 %copy-start.1 = (bf16[256,256]{1,0:T(8,128)(2,1)S(1)}, bf16[256,256]{1,0:T(8,128)(2,1)}, u32[]{:S(2)}) copy-start(bf16[256,256]{1,0:T(8,128)(2,1)} %get-tuple-element.371) | copy-start | bytes 393220 | tf_op jit(solution)/shard_map/while
  39.2 4.0 %copy-start.1 = (bf16[256,256]{1,0:T(8,128)(2,1)S(1)}, bf16[256,256]{1,0:T(8,128)(2,1)}, u32[]{:S(2)}) copy-start(bf16[256,256]{1,0:T(8,128)(2,1)} %get-tuple-element.371) | copy-start | bytes 393220 | tf_op jit(solution)/shard_map/while
  44.3 4.0 %copy-start.1 = (bf16[256,256]{1,0:T(8,128)(2,1)S(1)}, bf16[256,256]{1,0:T(8,128)(2,1)}, u32[]{:S(2)}) copy-start(bf16[256,256]{1,0:T(8,128)(2,1)} %get-tuple-element.371) | copy-start | bytes 393220 | tf_op jit(solution)/shard_map/while
  49.3 4.1 %copy-start.1 = (bf16[256,256]{1,0:T(8,128)(2,1)S(1)}, bf16[256,256]{1,0:T(8,128)(2,1)}, u32[]{:S(2)}) copy-start(bf16[256,256]{1,0:T(8,128)(2,1)} %get-tuple-element.371) | copy-start | bytes 393220 | tf_op jit(solution)/shard_map/while
  54.3 4.0 %copy-start.1 = (bf16[256,256]{1,0:T(8,128)(2,1)S(1)}, bf16[256,256]{1,0:T(8,128)(2,1)}, u32[]{:S(2)}) copy-start(bf16[256,256]{1,0:T(8,128)(2,1)} %get-tuple-element.371) | copy-start | bytes 393220 | tf_op jit(solution)/shard_map/while
  59.3 4.0 %copy-start.1 = (bf16[256,256]{1,0:T(8,128)(2,1)S(1)}, bf16[256,256]{1,0:T(8,128)(2,1)}, u32[]{:S(2)}) copy-start(bf16[256,256]{1,0:T(8,128)(2,1)} %get-tuple-element.371) | copy-start | bytes 393220 | tf_op jit(solution)/shard_map/while
  64.4 4.0 %copy-start.1 = (bf16[256,256]{1,0:T(8,128)(2,1)S(1)}, bf16[256,256]{1,0:T(8,128)(2,1)}, u32[]{:S(2)}) copy-start(bf16[256,256]{1,0:T(8,128)(2,1)} %get-tuple-element.371) | copy-start | bytes 393220 | tf_op jit(solution)/shard_map/while
  69.4 4.0 %copy-start.1 = (bf16[256,256]{1,0:T(8,128)(2,1)S(1)}, bf16[256,256]{1,0:T(8,128)(2,1)}, u32[]{:S(2)}) copy-start(bf16[256,256]{1,0:T(8,128)(2,1)} %get-tuple-element.371) | copy-start | bytes 393220 | tf_op jit(solution)/shard_map/while
  74.4 4.0 %copy-start.1 = (bf16[256,256]{1,0:T(8,128)(2,1)S(1)}, bf16[256,256]{1,0:T(8,128)(2,1)}, u32[]{:S(2)}) copy-start(bf16[256,256]{1,0:T(8,128)(2,1)} %get-tuple-element.371) | copy-start | bytes 393220 | tf_op jit(solution)/shard_map/while
  79.4 4.0 %copy-start.1 = (bf16[256,256]{1,0:T(8,128)(2,1)S(1)}, bf16[256,256]{1,0:T(8,128)(2,1)}, u32[]{:S(2)}) copy-start(bf16[256,256]{1,0:T(8,128)(2,1)} %get-tuple-element.371) | copy-start | bytes 393220 | tf_op jit(solution)/shard_map/while
  84.4 4.0 %copy-start.1 = (bf16[256,256]{1,0:T(8,128)(2,1)S(1)}, bf16[256,256]{1,0:T(8,128)(2,1)}, u32[]{:S(2)}) copy-start(bf16[256,256]{1,0:T(8,128)(2,1)} %get-tuple-element.371) | copy-start | bytes 393220 | tf_op jit(solution)/shard_map/while
  184.3 12.7 %copy-start.3 = (bf16[16,256,256]{2,1,0:T(8,128)(2,1)S(1)}, bf16[16,256,256]{2,1,0:T(8,128)(2,1)}, u32[]{:S(2)}) copy-start(bf16[16,256,256]{2,1,0:T(8,128)(2,1)} %get-tuple-element.96) | copy-start | bytes 6291460
  202.2 10.8 %all-to-all-start.1 = ((f32[16,1,1024]{2,1,0:T(1,128)}), f32[16,1,1024]{2,1,0:T(1,128)S(1)}, u32[]{:S(2)}, u32[]{:S(2)}) async-start(f32[16,1,1024]{2,1,0:T(1,128)} %reshape.132), calls=%async_computation.1 | async-start | bytes 131072 | tf_op jit(solution)/shard_map/all_to_all | solution.py:109
  213.0 10.4 %all-to-all-start.2 = ((f32[16,1,1024]{2,1,0:T(1,128)}), f32[16,1,1024]{2,1,0:T(1,128)S(1)}, u32[]{:S(2)}, u32[]{:S(2)}) async-start(f32[16,1,1024]{2,1,0:T(1,128)} %reshape.134), calls=%async_computation.2 | async-start | bytes 131072 | tf_op jit(solution)/shard_map/all_to_all | solution.py:110
  219.7 10.6 %copy-start.7 = (bf16[512]{0:T(512)(128)(2,1)S(1)}, bf16[512]{0:T(512)(128)(2,1)}, u32[]{:S(2)}) copy-start(bf16[512]{0:T(512)(128)(2,1)} %param.29) | copy-start | bytes 3076
  223.3 54.5 %all-to-all-start = ((bf16[16,1,16,16,256]{4,3,2,1,0:T(8,128)(2,1)}), bf16[16,1,16,16,256]{4,3,2,1,0:T(8,128)(2,1)}, u32[]{:S(2)}, u32[]{:S(2)}) async-start(bf16[16,1,16,16,256]{4,3,2,1,0:T(8,128)(2,1)} %fusion.29), calls=%async_computation | async-start | bytes 4194304 | tf_op jit(solution)/shard_map/all_to_all | solution.py:98
  (36 other events, 98.2 us)
Sparse Core Ops, SparseCore 0:
  10.7 42.2 all-gather.1
